TPU v7x, 32 devices: a whole 2x2x4 slice. The times are simulated.
32 devices in a mesh: grp: 4 (over y, x), dev: 8 (over z, core).
Axes of the slice: x: 2, y: 2, z: 4, core: 2. Of those that a mesh axis runs over, the one named last changes fastest.
Arguments:
- acts: bfloat16 [8192, 12288], P(('grp', 'dev')), may hold values from -6 to 6
- grads_out: bfloat16 [8192, 64], P(('grp', 'dev')), may hold values from -0.375 to 0.375
- residual_in: float32 [32, 64, 12288], P(('grp', 'dev')), may hold values from -6 to 6
- sel_index: int32 [32, 64], P(('grp', 'dev')), may hold values from 0 to 6143, as said below
- sel_count: int32 [32], P(('grp', 'dev')), may hold values from 16 to 64, as said below
- momentum_in: float32 [64, 12288], P(None, 'dev'), may hold values from -6 to 6
Outputs:
- residual_out: float32 [32, 64, 12288], P(('grp', 'dev'))
- momentum_out: float32 [64, 12288], P(None, 'dev')
Inputs may be any that keep to these rules, and one draw needn't show every extreme that they name: `sel_index`: the 64 numbers of a row are distinct. `sel_count`: equal to 64 on some device in every draw.
All inputs are finite; a program needn't handle non-finite values.
Results may differ from a plain program's by a relative error of at most 0.0003.
Values sent between devices are 32-bit elements; how exact they have to be, the bound alone decides.
A program may use at most 64 MiB of HBM per device.

v0:
```python
import jax
import jax.numpy as jnp
from jax import lax
from jax.sharding import PartitionSpec as P

momentum_decay = 0.9


def from_behind(block, axis, distance):
    devices = range(lax.axis_size(axis))
    route = [((i - distance) % len(devices), i) for i in devices]
    return lax.ppermute(block, axis, route)


def local(acts, grads_out, residual_in, sel_index, sel_count, momentum_in):
    width = acts.shape[1]
    columns = grads_out.shape[1]
    slots = sel_index.shape[1]
    n_blocks = columns * width // 128
    part_width = momentum_in.shape[1]
    local_grad = lax.dot_general(
        grads_out, acts, (((0,), (0,)), ((), ())), preferred_element_type=jnp.float32
    )
    summed = residual_in[0] + local_grad
    blocks = summed.reshape(n_blocks, 128)
    chosen = sel_index[0]
    valid_rows = (jnp.arange(slots, dtype=jnp.int32) < sel_count[0]).astype(jnp.float32)
    picked = blocks[chosen] * valid_rows[:, None]
    marked = jnp.zeros((n_blocks,), jnp.float32).at[chosen].max(valid_rows)
    kept = (blocks * (1.0 - marked)[:, None]).reshape(1, columns, width)
    labels = chosen.astype(jnp.float32)
    group_vals, group_labels = (
        lax.all_gather(picked, "dev", axis=0, tiled=True),
        lax.all_gather(labels, "dev", axis=0, tiled=True),
    )
    n_groups = lax.axis_size("grp")
    here = lax.axis_index("grp")
    store_vals = jnp.zeros((n_groups,) + group_vals.shape, jnp.float32)
    store_labels = jnp.zeros((n_groups,) + group_labels.shape, jnp.float32)
    store_vals = lax.dynamic_update_index_in_dim(store_vals, group_vals, here, 0)
    store_labels = lax.dynamic_update_index_in_dim(store_labels, group_labels, here, 0)

    def advance(rounds, carry):
        moving_vals, moving_labels, kept_vals, kept_labels = carry
        moving_vals, moving_labels = from_behind((moving_vals, moving_labels), "grp", 1)
        source = (here - rounds) % n_groups
        kept_vals = lax.dynamic_update_index_in_dim(kept_vals, moving_vals, source, 0)
        kept_labels = lax.dynamic_update_index_in_dim(kept_labels, moving_labels, source, 0)
        return (moving_vals, moving_labels, kept_vals, kept_labels)

    carried = lax.fori_loop(
        1, n_groups, advance, (group_vals, group_labels, store_vals, store_labels)
    )
    all_vals = carried[2].reshape(-1, 128)
    all_labels = carried[3].reshape(-1).astype(jnp.int32)
    spread = (
        jnp.zeros((n_blocks, 128), jnp.float32).at[all_labels].add(all_vals).reshape(columns, width)
    )
    total = lax.dynamic_slice_in_dim(spread, lax.axis_index("dev") * part_width, part_width, 1)
    momentum_out = momentum_decay * momentum_in + total
    return (kept, momentum_out)


def solution(mesh):
    placed = (
        P(("grp", "dev"), None),
        P(("grp", "dev"), None),
        P(("grp", "dev"), None, None),
        P(("grp", "dev"), None),
        P(("grp", "dev")),
        P(None, "dev"),
    )
    return jax.shard_map(
        local,
        mesh=mesh,
        in_specs=placed,
        out_specs=(P(("grp", "dev"), None, None), P(None, "dev")),
        check_vma=False,
    )
```

profile of v0, /device:TPU:0, one launch (start us, length us, event | category | flops | bytes accessed | tf_op | source)
XLA Modules:
  0.0 100.5 jit_solution(11768598687038377532)
XLA Ops:
  0.7 0.7 copy-done
  1.4 4.9 %convolution_add_fusion = f32[64,12288]{1,0:T(8,128)S(1)} fusion(bf16[256,64]{0,1:T(8,128)(2,1)S(1)} %copy-done, bf16[256,12288]{1,0:T(8,128)(2,1)} %param.8, f32[1,64,12288]{2,1,0:T(8,128)} %param.10), kind=kOutput, calls=%fused_computation.4 | convolution fusion | flops 403439616 | bytes 12615680 | tf_op jit(solution)/shard_map/dot_general | solution.py:21
  6.3 1.9 %reshape.79 = f32[6144,128]{1,0:T(8,128)} reshape(f32[64,12288]{1,0:T(8,128)S(1)} %convolution_add_fusion) | data formatting | bytes 6291456 | tf_op jit(solution)/shard_map/reshape | solution.py:25
  8.3 2.5 %gather_fusion = f32[64,128]{1,0:T(8,128)S(1)} fusion(f32[6144,128]{1,0:T(8,128)} %reshape.79, s32[1024]{0:T(1024)S(1)} %pad_clamp_fusion), kind=kCustom, calls=%fused_computation | custom fusion | bytes 65792 | tf_op jit(solution)/shard_map/gather | solution.py:28
  11.5 15.9 %all_gather.6 = f32[512,128]{1,0:T(8,128)S(1)} all-gather(f32[64,128]{1,0:T(8,128)S(1)} %broadcast_multiply_fusion), channel_id=1, replica_groups=mesh['grp'=4,'dev'=8] {'dev'}, dimensions={0}, use_global_device_ids=true | all-gather | bytes 294912 | tf_op jit(solution)/shard_map/all_gather | solution.py:33
  28.1 1.0 copy-done.2
  30.5 16.9 %all-reduce = f32[512]{0:T(512)S(1)} all-reduce(f32[512]{0:T(512)S(1)} %bitcast_dynamic-update-slice_fusion.2), channel_id=2, replica_groups=mesh['grp'=4,'dev'=8] {'dev'}, use_global_device_ids=true, to_apply=%add | all-reduce | flops 512 | bytes 4096 | tf_op jit(solution)/shard_map/all_gather | solution.py:34
  47.4 27.6 %while.21 = (s32[]{:T(128)}, f32[512,128]{1,0:T(8,128)}, f32[512]{0:T(512)S(1)}, f32[4,512,128]{2,1,0:T(8,128)}, f32[4,512]{1,0:T(4,128)S(1)}, /*index=5*/s32[]{:T(128)}, s32[]{:T(128)}, s32[]{:T(128)}, s32[]{:T(128)}, s32[]{:T(128)}) while((s32[]{:T(128)}, f32[512,128]{1,0:T(8,128)}, f32[512]{0:T(512)S(1)}, f32[4,512,128]{2,1,0:T(8,128)}, ...), condition=%wide.region_2.3_spmd, body=%wide.region_1.2_spmd.sunk | while | flops 17 | bytes 2113880 | solution.py:51
  47.4 1.5 %collective-permute-start = (f32[512,128]{1,0:T(8,128)}, f32[512,128]{1,0:T(8,128)S(1)}, u32[]{:S(2)}, u32[]{:S(2)}) collective-permute-start(f32[512,128]{1,0:T(8,128)} %get-tuple-element.220), channel_id=1, source_target_pairs={{24,0},{0,8},{8,16},{16,24},{25,1},{1,9},{9,17},{17,25},{26,2},{2,... | collective-permute-start | bytes 786440 | tf_op jit(solution)/shard_map/while/body/eval_jaxpr/ppermute | solution.py:12
  49.0 1.5 %collective-permute-start.1 = (f32[512]{0:T(512)S(1)}, f32[512]{0:T(512)S(1)}, u32[]{:S(2)}, u32[]{:S(2)}) collective-permute-start(f32[512]{0:T(512)S(1)} %get-tuple-element.221), channel_id=1, source_target_pairs={{24,0},{0,8},{8,16},{16,24},{25,1},{1,9},{9,17},{17,25},{26,2},{2,... | collective-permute-start | bytes 6152 | tf_op jit(solution)/shard_map/while/body/eval_jaxpr/ppermute | solution.py:12
  50.5 4.5 %collective-permute-done.1 = f32[512]{0:T(512)S(1)} collective-permute-done((f32[512]{0:T(512)S(1)}, f32[512]{0:T(512)S(1)}, u32[]{:S(2)}, u32[]{:S(2)}) %collective-permute-start.1) | collective-permute-done | bytes 2080 | tf_op jit(solution)/shard_map/while/body/eval_jaxpr/ppermute | solution.py:12
  55.8 0.7 bitcast_dynamic-update-slice_fusion.4
  56.5 0.9 collective-permute-start
  57.4 2.0 %collective-permute-start.1 = (f32[512]{0:T(512)S(1)}, f32[512]{0:T(512)S(1)}, u32[]{:S(2)}, u32[]{:S(2)}) collective-permute-start(f32[512]{0:T(512)S(1)} %get-tuple-element.221), channel_id=1, source_target_pairs={{24,0},{0,8},{8,16},{16,24},{25,1},{1,9},{9,17},{17,25},{26,2},{2,... | collective-permute-start | bytes 6152 | tf_op jit(solution)/shard_map/while/body/eval_jaxpr/ppermute | solution.py:12
  59.5 5.1 %collective-permute-done.1 = f32[512]{0:T(512)S(1)} collective-permute-done((f32[512]{0:T(512)S(1)}, f32[512]{0:T(512)S(1)}, u32[]{:S(2)}, u32[]{:S(2)}) %collective-permute-start.1) | collective-permute-done | bytes 2080 | tf_op jit(solution)/shard_map/while/body/eval_jaxpr/ppermute | solution.py:12
  65.3 0.7 bitcast_dynamic-update-slice_fusion.4
  66.7 2.3 %collective-permute-start.1 = (f32[512]{0:T(512)S(1)}, f32[512]{0:T(512)S(1)}, u32[]{:S(2)}, u32[]{:S(2)}) collective-permute-start(f32[512]{0:T(512)S(1)} %get-tuple-element.221), channel_id=1, source_target_pairs={{24,0},{0,8},{8,16},{16,24},{25,1},{1,9},{9,17},{17,25},{26,2},{2,... | collective-permute-start | bytes 6152 | tf_op jit(solution)/shard_map/while/body/eval_jaxpr/ppermute | solution.py:12
  69.0 4.5 %collective-permute-done.1 = f32[512]{0:T(512)S(1)} collective-permute-done((f32[512]{0:T(512)S(1)}, f32[512]{0:T(512)S(1)}, u32[]{:S(2)}, u32[]{:S(2)}) %collective-permute-start.1) | collective-permute-done | bytes 2080 | tf_op jit(solution)/shard_map/while/body/eval_jaxpr/ppermute | solution.py:12
  75.1 13.6 %scatter_custom_fusion.1 = f32[6144,128]{1,0:T(8,128)} fusion(s32[2048]{0:T(1024)S(1)} %bitcast.41, f32[2048,128]{1,0:T(8,128)} %bitcast.38, f32[]{:T(128)} %constant.79.clone.1), kind=kCustom, calls=%fused_computation.7 | custom fusion | flops 262144 | bytes 3146240 | tf_op jit(solution)/shard_map/scatter-add | solution.py:57
  88.7 4.3 %reshape.81 = f32[64,12288]{1,0:T(8,128)} reshape(f32[6144,128]{1,0:T(8,128)} %scatter_custom_fusion.1) | data formatting | bytes 6291456 | tf_op jit(solution)/shard_map/reshape | solution.py:57
  93.0 1.9 %dynamic-slice_add_fusion = f32[64,1536]{1,0:T(8,128)} fusion(f32[64,12288]{1,0:T(8,128)} %reshape.81, s32[]{:T(128)S(6)} %select_n.64, f32[64,1536]{1,0:T(8,128)} %param.13), kind=kLoop, calls=%fused_computation.9 | loop fusion | flops 196608 | bytes 1179652 | tf_op jit(solution)/shard_map/add | solution.py:60
  94.9 0.9 scatter_custom_fusion
  96.0 0.9 mul.34
  96.8 3.6 %fusion = f32[1,64,12288]{2,1,0:T(8,128)} fusion(f32[64,12288]{1,0:T(8,128)S(1)} %convolution_add_fusion, f32[8,8,96,128]{3,2,1,0:T(8,128)S(1)} %bitcast.37), kind=kLoop, calls=%fused_computation.6 | loop fusion | flops 786432 | bytes 9437184 | tf_op jit(solution)/shard_map/mul | solution.py:30
  (38 shorter events, 5.3 us)
Async XLA Ops:
  0.6 0.8 copy-start
  6.3 1.9 %copy-start.3 = (s32[1,64]{1,0:T(1,128)S(1)}, s32[1,64]{1,0:T(1,128)}, u32[]{:S(2)}) copy-start(s32[1,64]{1,0:T(1,128)} %param.11) | copy-start | bytes 772
  6.3 22.8 %copy-start.4 = (u32[32]{0:T(128)S(1)}, u32[32]{0:T(128)}, u32[]{:S(2)}) copy-start(u32[32]{0:T(128)} %constant.93) | copy-start | bytes 388
  27.4 0.7 copy-start.1
  28.1 1.0 copy-start.2
  47.4 7.6 %collective-permute-start = (f32[512,128]{1,0:T(8,128)}, f32[512,128]{1,0:T(8,128)S(1)}, u32[]{:S(2)}, u32[]{:S(2)}) collective-permute-start(f32[512,128]{1,0:T(8,128)} %get-tuple-element.220), channel_id=1, source_target_pairs={{24,0},{0,8},{8,16},{16,24},{25,1},{1,9},{9,17},{17,25},{26,2},{2,... | collective-permute-start | bytes 786440 | tf_op jit(solution)/shard_map/while/body/eval_jaxpr/ppermute | solution.py:12
  49.0 6.0 %collective-permute-start.1 = (f32[512]{0:T(512)S(1)}, f32[512]{0:T(512)S(1)}, u32[]{:S(2)}, u32[]{:S(2)}) collective-permute-start(f32[512]{0:T(512)S(1)} %get-tuple-element.221), channel_id=1, source_target_pairs={{24,0},{0,8},{8,16},{16,24},{25,1},{1,9},{9,17},{17,25},{26,2},{2,... | collective-permute-start | bytes 6152 | tf_op jit(solution)/shard_map/while/body/eval_jaxpr/ppermute | solution.py:12
  56.5 8.1 %collective-permute-start = (f32[512,128]{1,0:T(8,128)}, f32[512,128]{1,0:T(8,128)S(1)}, u32[]{:S(2)}, u32[]{:S(2)}) collective-permute-start(f32[512,128]{1,0:T(8,128)} %get-tuple-element.220), channel_id=1, source_target_pairs={{24,0},{0,8},{8,16},{16,24},{25,1},{1,9},{9,17},{17,25},{26,2},{2,... | collective-permute-start | bytes 786440 | tf_op jit(solution)/shard_map/while/body/eval_jaxpr/ppermute | solution.py:12
  57.4 7.2 %collective-permute-start.1 = (f32[512]{0:T(512)S(1)}, f32[512]{0:T(512)S(1)}, u32[]{:S(2)}, u32[]{:S(2)}) collective-permute-start(f32[512]{0:T(512)S(1)} %get-tuple-element.221), channel_id=1, source_target_pairs={{24,0},{0,8},{8,16},{16,24},{25,1},{1,9},{9,17},{17,25},{26,2},{2,... | collective-permute-start | bytes 6152 | tf_op jit(solution)/shard_map/while/body/eval_jaxpr/ppermute | solution.py:12
  66.1 7.6 %collective-permute-start = (f32[512,128]{1,0:T(8,128)}, f32[512,128]{1,0:T(8,128)S(1)}, u32[]{:S(2)}, u32[]{:S(2)}) collective-permute-start(f32[512,128]{1,0:T(8,128)} %get-tuple-element.220), channel_id=1, source_target_pairs={{24,0},{0,8},{8,16},{16,24},{25,1},{1,9},{9,17},{17,25},{26,2},{2,... | collective-permute-start | bytes 786440 | tf_op jit(solution)/shard_map/while/body/eval_jaxpr/ppermute | solution.py:12
  66.7 6.8 %collective-permute-start.1 = (f32[512]{0:T(512)S(1)}, f32[512]{0:T(512)S(1)}, u32[]{:S(2)}, u32[]{:S(2)}) collective-permute-start(f32[512]{0:T(512)S(1)} %get-tuple-element.221), channel_id=1, source_target_pairs={{24,0},{0,8},{8,16},{16,24},{25,1},{1,9},{9,17},{17,25},{26,2},{2,... | collective-permute-start | bytes 6152 | tf_op jit(solution)/shard_map/while/body/eval_jaxpr/ppermute | solution.py:12
where the time goes:
time: 101 us; the launch traced here: 100 us
  blocking collectives  32.8 us (32%)
  other arithmetic  20.3 us (20%)
  local copies, waits for them, and re-layouts  17.1 us (17%)
  waiting for transfers between devices  14.2 us (14%)
  starting transfers between devices  8.97 us (9%)
  matrix products  4.91 us (5%)
  between operations  2.04 us (2%)
    all_gather x1, blocking collectives, local(): lax.all_gather(labels, 'dev', axis=0, tiled=True)  16.9 us
    all_gather x1, blocking collectives, local(): lax.all_gather(picked, 'dev', axis=0, tiled=True)  15.9 us
    ppermute x6, waiting for transfers between devices, from_behind(): return lax.ppermute(block, axis, route)  14.2 us
    scatter-add x1, other arithmetic, local(): jnp.zeros((n_blocks, 128), jnp.float32).at[all_labels].add(all_vals)  13.6 us
    ppermute x6, starting transfers between devices, from_behind(): return lax.ppermute(block, axis, route)  8.97 us
    dot_general x1, matrix products, local(): lax.dot_general(grads_out, acts, (((0,), (0,)), ((), ())), preferred_elem...  4.91 us
    reshape x1, local copies, waits for them, and re-layouts, local(): jnp.zeros((n_blocks, 128), jnp.float32).at[all_labels].add(all_vals)  4.3 us
    mul x1, other arithmetic, local(): kept = (blocks * (1.0 - marked)[:, None]).reshape(1, columns, width)  3.64 us
  transfers between devices with their start and end apart: 6, of which 3 were waited for; matrix products, arithmetic and copies ran while one was open for 0% of the time, Pallas kernels for 0%

commit v1 on v0

--- a/solution.py
+++ b/solution.py
@@ -31,7 +31,9 @@
     labels = chosen.astype(jnp.float32)
     group_vals, group_labels = (
         lax.all_gather(picked, "dev", axis=0, tiled=True),
-        lax.all_gather(labels, "dev", axis=0, tiled=True),
+        jnp.concatenate(
+            lax.all_to_all(jnp.stack([labels] * lax.axis_size("dev")), "dev", 0, 0), axis=0
+        ),
     )
     n_groups = lax.axis_size("grp")
     here = lax.axis_index("grp")

time: 101 us -> 85 us (0.84)
  blocking collectives: 32.8 us -> 14.7 us
  local copies, waits for them, and re-layouts: 17.1 us -> 9.91 us
  starting transfers between devices: 8.97 us -> 15.4 us
  waiting for transfers between devices: 14.2 us -> 17 us
    all_gather x1 -> x0, blocking collectives: 16.9 us -> none  [local(): lax.all_gather(labels, 'dev', axis=0, tiled=True)]
    all_to_all x0 -> x1, starting transfers between devices: none -> 6.35 us  [local(): lax.all_to_all(jnp.stack([labels] * lax.axis_size('dev')), 'dev', 0, 0)]
    ppermute x6, waiting for transfers between devices: 14.2 us -> 17 us  [from_behind(): return lax.ppermute(block, axis, route)]
    reshape x1, local copies, waits for them, and re-layouts: 4.3 us -> 1.97 us  [local(): jnp.zeros((n_blocks, 128), jnp.float32).at[all_labels].add(all_vals)]
    dynamic_update_slice x3, local copies, waits for them, and re-layouts: 2.16 us -> 0.07 us  [advance(): lax.dynamic_update_index_in_dim(kept_vals, moving_vals, source, 0)]
    while x6, local copies, waits for them, and re-layouts: 2.12 us -> 0.06 us
    unnamed x13 -> x5, local copies, waits for them, and re-layouts: 2.97 us -> 0.95 us
    all_gather x1, blocking collectives: 15.9 us -> 14.7 us  [local(): lax.all_gather(picked, 'dev', axis=0, tiled=True)]
  transfers between devices with their start and end apart: 6 -> 7, of which waited for: 3 -> 3; matrix products, arithmetic and copies ran while one was open for 0% -> 19% of each run, Pallas kernels for 0% -> 0%
where the time goes in v1:
time: 85 us; the launch traced here: 84.7 us
  other arithmetic  21.1 us (25%)
  waiting for transfers between devices  17 us (20%)
  starting transfers between devices  15.4 us (18%)
  blocking collectives  14.7 us (17%)
  local copies, waits for them, and re-layouts  9.91 us (12%)
  matrix products  4.91 us (6%)
  between operations  1.41 us (2%)
    ppermute x6, waiting for transfers between devices, from_behind(): return lax.ppermute(block, axis, route)  17 us
    all_gather x1, blocking collectives, local(): lax.all_gather(picked, 'dev', axis=0, tiled=True)  14.7 us
    scatter-add x1, other arithmetic, local(): jnp.zeros((n_blocks, 128), jnp.float32).at[all_labels].add(all_vals)  12.6 us
    ppermute x6, starting transfers between devices, from_behind(): return lax.ppermute(block, axis, route)  9.09 us
    all_to_all x1, starting transfers between devices, local(): lax.all_to_all(jnp.stack([labels] * lax.axis_size('dev')), 'dev', 0, 0)  6.35 us
    dot_general x1, matrix products, local(): lax.dot_general(grads_out, acts, (((0,), (0,)), ((), ())), preferred_elem...  4.91 us
    mul x1, other arithmetic, local(): kept = (blocks * (1.0 - marked)[:, None]).reshape(1, columns, width)  3.64 us
    gather x1, local copies, waits for them, and re-layouts, local(): picked = blocks[chosen] * valid_rows[:, None]  2.49 us
  transfers between devices with their start and end apart: 7, of which 3 were waited for; matrix products, arithmetic and copies ran while one was open for 19% of the time, Pallas kernels for 0%

profile of v1, /device:TPU:0, one launch (start us, length us, event | category | flops | bytes accessed | tf_op | source)
XLA Modules:
  0.0 84.7 jit_solution(4638347930431029947)
XLA Ops:
  0.6 0.7 convert_bitcast_fusion.1
  1.9 6.4 %all-to-all-start = ((f32[8,1,64]{2,1,0:T(1,128)}), f32[8,1,64]{2,1,0:T(1,128)S(1)}, u32[]{:S(2)}, u32[]{:S(2)}) async-start(f32[8,1,64]{2,1,0:T(1,128)} %stack.2), calls=%async_computation | async-start | bytes 8192 | tf_op jit(solution)/shard_map/all_to_all | solution.py:35
  8.3 0.7 fusion.5
  8.9 4.9 %convolution_add_fusion = f32[64,12288]{1,0:T(8,128)S(1)} fusion(bf16[256,64]{0,1:T(8,128)(2,1)S(1)} %copy-done, bf16[256,12288]{1,0:T(8,128)(2,1)} %param.8, f32[1,64,12288]{2,1,0:T(8,128)} %param.10), kind=kOutput, calls=%fused_computation.4 | convolution fusion | flops 403439616 | bytes 12615680 | tf_op jit(solution)/shard_map/dot_general | solution.py:21
  13.8 1.9 %reshape.91 = f32[6144,128]{1,0:T(8,128)} reshape(f32[64,12288]{1,0:T(8,128)S(1)} %convolution_add_fusion) | data formatting | bytes 6291456 | tf_op jit(solution)/shard_map/reshape | solution.py:25
  16.4 2.5 %gather_fusion = f32[64,128]{1,0:T(8,128)S(1)} fusion(f32[6144,128]{1,0:T(8,128)} %reshape.91, s32[1024]{0:T(1024)S(1)} %pad_clamp_fusion), kind=kCustom, calls=%fused_computation | custom fusion | bytes 65792 | tf_op jit(solution)/shard_map/gather | solution.py:28
  19.0 14.7 %all_gather.3 = f32[512,128]{1,0:T(8,128)S(1)} all-gather(f32[64,128]{1,0:T(8,128)S(1)} %broadcast_multiply_fusion), channel_id=1, replica_groups=mesh['grp'=4,'dev'=8] {'dev'}, dimensions={0}, use_global_device_ids=true | all-gather | bytes 294912 | tf_op jit(solution)/shard_map/all_gather | solution.py:33
  33.7 0.9 %scatter_custom_fusion = f32[6144]{0:T(1024)S(1)} fusion(s32[64]{0:T(128)S(1)} %fusion.5, f32[64]{0:T(128)S(1)} %compare_convert_fusion, f32[]{:T(128)} %constant.79.clone.1), kind=kCustom, calls=%fused_computation.13 | custom fusion | flops 64 | bytes 24580 | tf_op jit(solution)/shard_map/scatter-max | solution.py:29
  34.7 0.9 %mul.34 = f32[64,96,128]{2,1,0:T(8,128)S(1)} broadcast(f32[64,96]{1,0:T(8,128)S(1)} %mul.33), dimensions={0,1} | broadcast | bytes 3170304 | tf_op jit(solution)/shard_map/mul | solution.py:30
  35.6 3.6 %fusion = f32[1,64,12288]{2,1,0:T(8,128)} fusion(f32[64,12288]{1,0:T(8,128)S(1)} %convolution_add_fusion, f32[8,8,96,128]{3,2,1,0:T(8,128)S(1)} %bitcast.36), kind=kLoop, calls=%fused_computation.6 | loop fusion | flops 786432 | bytes 9437184 | tf_op jit(solution)/shard_map/mul | solution.py:30
  40.0 0.7 reduce.5
  40.8 26.5 %while.21 = (s32[]{:T(128)}, f32[512,128]{1,0:T(8,128)S(1)}, f32[512]{0:T(512)S(1)}, f32[4,512,128]{2,1,0:T(8,128)S(1)}, f32[4,512]{1,0:T(4,128)S(1)}, /*index=5...) while((s32[]{:T(128)}, f32[512,128]{1,0:T(8,128)S(1)}, f32[512]{0:T(512)S(1)}, ...), condition=%wide.region_2.3_spmd, body=%wide.region_1.2_spmd.sunk | while | flops 17 | bytes 2113880 | solution.py:53
  40.8 1.5 %collective-permute-start = (f32[512,128]{1,0:T(8,128)S(1)}, f32[512,128]{1,0:T(8,128)S(1)}, u32[]{:S(2)}, u32[]{:S(2)}) collective-permute-start(f32[512,128]{1,0:T(8,128)S(1)} %get-tuple-element.220), channel_id=1, source_target_pairs={{24,0},{0,8},{8,16},{16,24},{25,1},{1,9},{9,17},{17,25},{26,2},{2,... | collective-permute-start | bytes 786440 | tf_op jit(solution)/shard_map/while/body/eval_jaxpr/ppermute | solution.py:12
  42.3 1.5 %collective-permute-start.1 = (f32[512]{0:T(512)S(1)}, f32[512]{0:T(512)S(1)}, u32[]{:S(2)}, u32[]{:S(2)}) collective-permute-start(f32[512]{0:T(512)S(1)} %get-tuple-element.221), channel_id=1, source_target_pairs={{24,0},{0,8},{8,16},{16,24},{25,1},{1,9},{9,17},{17,25},{26,2},{2,... | collective-permute-start | bytes 6152 | tf_op jit(solution)/shard_map/while/body/eval_jaxpr/ppermute | solution.py:12
  43.8 6.5 %collective-permute-done.1 = f32[512]{0:T(512)S(1)} collective-permute-done((f32[512]{0:T(512)S(1)}, f32[512]{0:T(512)S(1)}, u32[]{:S(2)}, u32[]{:S(2)}) %collective-permute-start.1) | collective-permute-done | bytes 2080 | tf_op jit(solution)/shard_map/while/body/eval_jaxpr/ppermute | solution.py:12
  50.4 0.6 collective-permute-start
  51.1 2.4 %collective-permute-start.1 = (f32[512]{0:T(512)S(1)}, f32[512]{0:T(512)S(1)}, u32[]{:S(2)}, u32[]{:S(2)}) collective-permute-start(f32[512]{0:T(512)S(1)} %get-tuple-element.221), channel_id=1, source_target_pairs={{24,0},{0,8},{8,16},{16,24},{25,1},{1,9},{9,17},{17,25},{26,2},{2,... | collective-permute-start | bytes 6152 | tf_op jit(solution)/shard_map/while/body/eval_jaxpr/ppermute | solution.py:12
  53.5 5.7 %collective-permute-done.1 = f32[512]{0:T(512)S(1)} collective-permute-done((f32[512]{0:T(512)S(1)}, f32[512]{0:T(512)S(1)}, u32[]{:S(2)}, u32[]{:S(2)}) %collective-permute-start.1) | collective-permute-done | bytes 2080 | tf_op jit(solution)/shard_map/while/body/eval_jaxpr/ppermute | solution.py:12
  59.3 3.0 %collective-permute-start.1 = (f32[512]{0:T(512)S(1)}, f32[512]{0:T(512)S(1)}, u32[]{:S(2)}, u32[]{:S(2)}) collective-permute-start(f32[512]{0:T(512)S(1)} %get-tuple-element.221), channel_id=1, source_target_pairs={{24,0},{0,8},{8,16},{16,24},{25,1},{1,9},{9,17},{17,25},{26,2},{2,... | collective-permute-start | bytes 6152 | tf_op jit(solution)/shard_map/while/body/eval_jaxpr/ppermute | solution.py:12
  62.3 4.8 %collective-permute-done.1 = f32[512]{0:T(512)S(1)} collective-permute-done((f32[512]{0:T(512)S(1)}, f32[512]{0:T(512)S(1)}, u32[]{:S(2)}, u32[]{:S(2)}) %collective-permute-start.1) | collective-permute-done | bytes 2080 | tf_op jit(solution)/shard_map/while/body/eval_jaxpr/ppermute | solution.py:12
  67.3 0.9 %copy-done.1 = f32[4,512,128]{2,1,0:T(8,128)} copy-done((f32[4,512,128]{2,1,0:T(8,128)}, f32[4,512,128]{2,1,0:T(8,128)S(1)}, u32[]{:S(2)}) %copy-start.1) | copy-done | bytes 1048600
  68.2 12.6 %scatter_custom_fusion.1 = f32[6144,128]{1,0:T(8,128)S(1)} fusion(s32[2048]{0:T(1024)S(1)} %bitcast.41, f32[2048,128]{1,0:T(8,128)} %bitcast.37, f32[]{:T(128)} %constant.79.clone.1), kind=kCustom, calls=%fused_computation.7 | custom fusion | flops 262144 | bytes 3146240 | tf_op jit(solution)/shard_map/scatter-add | solution.py:59
  80.8 2.0 %reshape.94 = f32[64,12288]{1,0:T(8,128)} reshape(f32[6144,128]{1,0:T(8,128)S(1)} %scatter_custom_fusion.1) | data formatting | bytes 6291456 | tf_op jit(solution)/shard_map/reshape | solution.py:59
  82.8 1.9 %dynamic-slice_add_fusion = f32[64,1536]{1,0:T(8,128)} fusion(f32[64,12288]{1,0:T(8,128)} %reshape.94, s32[]{:T(128)S(6)} %select_n.64, f32[64,1536]{1,0:T(8,128)} %param.13), kind=kLoop, calls=%fused_computation.9 | loop fusion | flops 196608 | bytes 1179652 | tf_op jit(solution)/shard_map/add | solution.py:62
  (36 shorter events, 1.9 us)
Async XLA Ops:
  0.6 8.3 %copy-start = (bf16[256,64]{0,1:T(8,128)(2,1)S(1)}, bf16[256,64]{0,1:T(8,128)(2,1)}, u32[]{:S(2)}) copy-start(bf16[256,64]{0,1:T(8,128)(2,1)} %param.9) | copy-start | bytes 98308
  1.9 37.5 %all-to-all-start = ((f32[8,1,64]{2,1,0:T(1,128)}), f32[8,1,64]{2,1,0:T(1,128)S(1)}, u32[]{:S(2)}, u32[]{:S(2)}) async-start(f32[8,1,64]{2,1,0:T(1,128)} %stack.2), calls=%async_computation | async-start | bytes 8192 | tf_op jit(solution)/shard_map/all_to_all | solution.py:35
  40.8 9.6 %collective-permute-start = (f32[512,128]{1,0:T(8,128)S(1)}, f32[512,128]{1,0:T(8,128)S(1)}, u32[]{:S(2)}, u32[]{:S(2)}) collective-permute-start(f32[512,128]{1,0:T(8,128)S(1)} %get-tuple-element.220), channel_id=1, source_target_pairs={{24,0},{0,8},{8,16},{16,24},{25,1},{1,9},{9,17},{17,25},{26,2},{2,... | collective-permute-start | bytes 786440 | tf_op jit(solution)/shard_map/while/body/eval_jaxpr/ppermute | solution.py:12
  42.3 8.0 %collective-permute-start.1 = (f32[512]{0:T(512)S(1)}, f32[512]{0:T(512)S(1)}, u32[]{:S(2)}, u32[]{:S(2)}) collective-permute-start(f32[512]{0:T(512)S(1)} %get-tuple-element.221), channel_id=1, source_target_pairs={{24,0},{0,8},{8,16},{16,24},{25,1},{1,9},{9,17},{17,25},{26,2},{2,... | collective-permute-start | bytes 6152 | tf_op jit(solution)/shard_map/while/body/eval_jaxpr/ppermute | solution.py:12
  50.4 8.7 %collective-permute-start = (f32[512,128]{1,0:T(8,128)S(1)}, f32[512,128]{1,0:T(8,128)S(1)}, u32[]{:S(2)}, u32[]{:S(2)}) collective-permute-start(f32[512,128]{1,0:T(8,128)S(1)} %get-tuple-element.220), channel_id=1, source_target_pairs={{24,0},{0,8},{8,16},{16,24},{25,1},{1,9},{9,17},{17,25},{26,2},{2,... | collective-permute-start | bytes 786440 | tf_op jit(solution)/shard_map/while/body/eval_jaxpr/ppermute | solution.py:12
  51.1 8.1 %collective-permute-start.1 = (f32[512]{0:T(512)S(1)}, f32[512]{0:T(512)S(1)}, u32[]{:S(2)}, u32[]{:S(2)}) collective-permute-start(f32[512]{0:T(512)S(1)} %get-tuple-element.221), channel_id=1, source_target_pairs={{24,0},{0,8},{8,16},{16,24},{25,1},{1,9},{9,17},{17,25},{26,2},{2,... | collective-permute-start | bytes 6152 | tf_op jit(solution)/shard_map/while/body/eval_jaxpr/ppermute | solution.py:12
  59.3 7.9 %collective-permute-start = (f32[512,128]{1,0:T(8,128)S(1)}, f32[512,128]{1,0:T(8,128)S(1)}, u32[]{:S(2)}, u32[]{:S(2)}) collective-permute-start(f32[512,128]{1,0:T(8,128)S(1)} %get-tuple-element.220), channel_id=1, source_target_pairs={{24,0},{0,8},{8,16},{16,24},{25,1},{1,9},{9,17},{17,25},{26,2},{2,... | collective-permute-start | bytes 786440 | tf_op jit(solution)/shard_map/while/body/eval_jaxpr/ppermute | solution.py:12
  59.3 7.8 %collective-permute-start.1 = (f32[512]{0:T(512)S(1)}, f32[512]{0:T(512)S(1)}, u32[]{:S(2)}, u32[]{:S(2)}) collective-permute-start(f32[512]{0:T(512)S(1)} %get-tuple-element.221), channel_id=1, source_target_pairs={{24,0},{0,8},{8,16},{16,24},{25,1},{1,9},{9,17},{17,25},{26,2},{2,... | collective-permute-start | bytes 6152 | tf_op jit(solution)/shard_map/while/body/eval_jaxpr/ppermute | solution.py:12
  67.2 1.0 %copy-start.1 = (f32[4,512,128]{2,1,0:T(8,128)}, f32[4,512,128]{2,1,0:T(8,128)S(1)}, u32[]{:S(2)}) copy-start(f32[4,512,128]{2,1,0:T(8,128)S(1)} %get-tuple-element.159) | copy-start | bytes 3145732
